TPU v7x, 32 devices: a whole 2x2x4 slice. The times are simulated.
32 devices in a mesh: dp: 8 (over z, x), cls: 4 (over y, core).
Axes of the slice: x: 2, y: 2, z: 4, core: 2. Of those that a mesh axis runs over, the one named last changes fastest.
Arguments:
- embeddings: bfloat16 [24576, 768], P('dp'), may hold values from -6 to 6
- labels: int32 [24576], P('dp'), may hold values from 0 to 2751, as said below
- row_count: int32 [8], P('dp'), may hold values from 768 to 3072
Outputs:
- class_means: float32 [2752, 768], P(('dp', 'cls'))
- prototypes: float32 [2752, 768], P(('dp', 'cls'))
- similarity: float32 [24576], P('dp')
Inputs may be any that keep to these rules, and one draw needn't show every extreme that they name: Rows of index i of dp at or beyond row_count[i] are padding. `labels`: classes c and c' belong to the same block when c // 86 == c' // 86; block b belongs to index b mod 4 of cls. The rows of one index of dp name at most 16 distinct classes of any one block. Some block has exactly 16 of its classes named by the rows of every index of dp. The rows of some index of dp name exactly 16 classes of every block of some index of cls.
All inputs are finite; a program needn't handle non-finite values.
Results may differ from a plain program's by a relative error of at most 0.0017.
Values sent between devices are 32-bit elements; how exact they have to be, the bound alone decides.
A program may use at most 64 MiB of HBM per device.

v0:
```python
import functools

import jax
import jax.numpy as jnp
from jax import lax
from jax.experimental import pallas as pl
from jax.experimental.pallas import tpu as pltpu
from jax.sharding import PartitionSpec as P

CLS_DEV = 86
SLOTS = 16
CLS_PAD = 128
CHUNK = 384
ROW_TILE = 512

epsilon = 1e-06
sharpness = 4.0

f32 = jnp.float32
bf16 = jnp.bfloat16
NN = (((1,), (0,)), ((), ()))
NT = (((1,), (1,)), ((), ()))


def dot(a, b, dims=NN):
    return lax.dot_general(a, b, dims, preferred_element_type=f32)


def split(x):
    hi = x.astype(bf16)
    return hi, (x - hi.astype(f32)).astype(bf16)


def iota(shape, dim):
    return lax.broadcasted_iota(jnp.int32, shape, dim).astype(f32)


def kernel(
    n,
    m,
    count_ref,
    label_ref,
    emb_ref,
    means_ref,
    proto_ref,
    sim_ref,
    emb,
    onehot,
    weighted_onehot,
    place_t,
    cnt_send,
    cnt_recv,
    a_send,
    a_recv,
    b_send,
    b_recv,
    c_send,
    c_recv,
    s_send,
    s_recv,
    dot_row,
    len_row,
    own,
    load_sem,
    cnt_ss,
    cnt_rs,
    big_ss,
    big_rs,
    s_ss,
    s_rs,
):
    rows = label_ref.shape[1]
    chunks = emb.shape[0]
    slots = n * SLOTS
    me = lax.axis_index("dp")
    mine = lax.axis_index("cls")
    half = n // 2
    height = half * SLOTS

    def index_of(g, z):
        return 2 * z + lax.rem(g + z, 2)

    my_z = me // 2
    my_position = lax.rem(my_z + me, 2) * half + my_z

    def partners(g):
        for off in range(half):
            z = lax.rem(my_z + off, half)
            yield index_of(g, z), g * half + z

    loads = []
    for f in range(chunks):
        load = pltpu.make_async_copy(
            emb_ref.at[:, pl.ds(f * CHUNK, CHUNK)], emb.at[f], load_sem.at[f]
        )
        load.start()
        loads.append(load)

    barrier = pltpu.get_barrier_semaphore()
    for off in range(1, n):
        pl.semaphore_signal(
            barrier, inc=1, device_id={"dp": lax.rem(me + off, n)}, device_id_type=pl.DeviceIdType.MESH
        )
    for off in range(1, m):
        pl.semaphore_signal(
            barrier, inc=1, device_id={"cls": lax.rem(mine + off, m)}, device_id_type=pl.DeviceIdType.MESH
        )

    label = label_ref[...].astype(f32)
    block = jnp.floor((label + 0.5) * (1.0 / CLS_DEV))
    place = label - CLS_DEV * block
    owner = jnp.floor((block + 0.5) * (1.0 / m))
    group = block - m * owner
    pair = jnp.floor(owner * 0.5)
    odd = pair + owner - 2.0 * jnp.floor((pair + owner) * 0.5)
    owner = odd * half + pair
    alive = lax.broadcasted_iota(jnp.int32, (1, rows), 1) < count_ref[0]
    owned = (group == mine.astype(f32)) & alive
    place = jnp.where(owned, place, -1.0)
    owner = jnp.where(owned, owner, -1.0)

    owner_mask = iota((n, rows), 0) == owner
    place_hot = jnp.where(iota((CLS_PAD, rows), 0) == place, 1.0, 0.0).astype(bf16)
    counts = dot(jnp.where(owner_mask, 1.0, 0.0).astype(bf16), place_hot, NT)
    upper = jnp.where(
        iota((CLS_PAD, CLS_PAD), 0) <= iota((CLS_PAD, CLS_PAD), 1), 1.0, 0.0
    ).astype(bf16)

    def ranks(table):
        return dot(jnp.where(table > 0, 1.0, 0.0).astype(bf16), upper) - 1.0

    for o in range(n):
        cnt_send[o] = jnp.broadcast_to(counts[o : o + 1, :], (8, CLS_PAD))
    cnt_recv[my_position] = cnt_send[my_position]

    rank_of = dot(ranks(counts).astype(bf16), place_hot) + SLOTS * iota((n, rows), 0)
    slot = jnp.sum(jnp.where(owner_mask, rank_of, 0.0), axis=0, keepdims=True)
    slot = jnp.where(owned, slot, -1.0)
    onehot[...] = jnp.where(iota((slots, rows), 0) == slot, 1.0, 0.0).astype(bf16)

    pl.semaphore_wait(barrier, n - 1 + m - 1)

    def dp_copy(src, dst, send_sem, recv_sem, target):
        return pltpu.make_async_remote_copy(
            src_ref=src,
            dst_ref=dst,
            send_sem=send_sem,
            recv_sem=recv_sem,
            device_id={"dp": target},
            device_id_type=pl.DeviceIdType.MESH,
        )

    def cnt_copy(target, to, frm):
        return dp_copy(cnt_send.at[to], cnt_recv.at[frm], cnt_ss.at[to], cnt_rs.at[frm], target)

    buffers = ((a_send, a_recv), (b_send, b_recv), (c_send, c_recv))

    def big_copy(phase, f, target, to, frm):
        send, recv = buffers[phase]
        return dp_copy(
            send.at[f, to], recv.at[f, frm], big_ss.at[phase, f, to], big_rs.at[phase, f, frm], target
        )

    def others(g, action):
        for target, to in partners(g):
            pl.when(target != me)(functools.partial(action, target, to))

    def send(phase, f, g):
        others(g, lambda target, to: big_copy(phase, f, target, to, my_position).start())

    def keep(phase, f):
        out, recv = buffers[phase]
        recv[f, my_position] = out[f, my_position]

    def arrived(phase, f, first, count):
        for p in range(first, first + count):
            pl.when(p != my_position)(lambda: big_copy(phase, f, me, p, p).wait_recv())
        recv = buffers[phase][1]
        return recv[f, first : first + count].reshape(count * SLOTS, CHUNK)

    for g in range(2):
        others(g, lambda target, to: cnt_copy(target, to, my_position).start())

    for f in range(chunks):
        loads[f].wait()
        a_send[f] = dot(onehot[...], emb[f]).reshape(n, SLOTS, CHUNK)
        send(0, f, 0)
        keep(0, f)
    for f in range(chunks):
        send(0, f, 1)

    for t in range(0, rows, ROW_TILE):
        squares = jnp.zeros((ROW_TILE, 128), f32)
        for f in range(chunks):
            for k in range(0, CHUNK, 128):
                x = emb[f, t : t + ROW_TILE, k : k + 128].astype(f32)
                squares = squares + x * x
        total = jnp.sum(jnp.transpose(squares), axis=0, keepdims=True)
        len_row[:, t : t + ROW_TILE] = jnp.sqrt(total + epsilon)

    for p in range(n):
        pl.when(p != my_position)(lambda: cnt_copy(me, p, p).wait_recv())
    table = jnp.concatenate([cnt_recv[i, 0:1, :] for i in range(n)], axis=0)
    table_rank = jnp.where(table > 0, ranks(table), -1.0)
    slot_iota = iota((SLOTS, CLS_PAD), 0)
    for i in range(n):
        place_t[i * SLOTS : (i + 1) * SLOTS, :] = jnp.where(
            table_rank[i : i + 1, :] == slot_iota, 1.0, 0.0
        )
    to_slots = place_t[...].astype(bf16)
    to_classes = jnp.transpose(place_t[...]).astype(bf16)
    own_counts = jnp.maximum(jnp.sum(table, axis=0, keepdims=True), 1.0)
    divisor = jnp.transpose(jnp.broadcast_to(own_counts, (CLS_PAD, CLS_PAD)))[:, 0:1]

    for f in range(chunks):
        hi, lo = split(arrived(0, f, 0, n))
        means = (dot(to_classes, hi) + dot(to_classes, lo)) / divisor
        hi, lo = split(means)
        b_send[f] = (dot(to_slots, hi) + dot(to_slots, lo)).reshape(n, SLOTS, CHUNK)
        send(1, f, 0)
        send(1, f, 1)
        keep(1, f)
        means_ref[:, f * CHUNK : (f + 1) * CHUNK] = means[:CLS_DEV, :]

    for g in range(2):
        span = slice(g * height, (g + 1) * height)
        norm = jnp.zeros((height, 1), f32)
        for f in range(chunks):
            mean = arrived(1, f, g * half, half)
            norm = norm + jnp.sum(mean * mean, axis=1, keepdims=True)
            both = jnp.concatenate(split(mean), axis=0)
            for t in range(0, rows, ROW_TILE):
                cols = slice(t, t + ROW_TILE)
                product = dot(both, emb[f, cols, :], NT)
                product = product[:height, :] + product[height:, :]
                product = jnp.sum(
                    product * onehot[span, cols].astype(f32), axis=0, keepdims=True
                )
                dot_row[:, cols] = product if f == 0 else dot_row[:, cols] + product
        scale = 1.0 / jnp.sqrt(norm + epsilon)
        for t in range(0, rows, ROW_TILE):
            cols = slice(t, t + ROW_TILE)
            hot = onehot[span, cols].astype(f32)
            row_scale = jnp.sum(hot * scale, axis=0, keepdims=True)
            similarity = dot_row[:, cols] * row_scale / len_row[:, cols]
            s_send[:, cols] = similarity if g == 0 else s_send[:, cols] + similarity
            weight = jnp.exp(sharpness * (similarity - 1.0))
            weighted_onehot[:, cols] = (hot * weight).astype(bf16)
        for f in range(chunks):
            c_send[f, g * half : (g + 1) * half] = dot(weighted_onehot[...], emb[f]).reshape(
                half, SLOTS, CHUNK
            )
            send(2, f, g)
    for f in range(chunks):
        keep(2, f)

    def s_copy(off):
        return pltpu.make_async_remote_copy(
            src_ref=s_send,
            dst_ref=s_recv.at[mine],
            send_sem=s_ss.at[off - 1],
            recv_sem=s_rs.at[off - 1],
            device_id={"cls": lax.rem(mine + off, m)},
            device_id_type=pl.DeviceIdType.MESH,
        )

    for off in range(1, m):
        s_copy(off).start()
    s_recv[mine] = s_send[...]
    for off in range(1, m):
        s_copy(off).wait_recv()
    full = s_recv[0]
    for j in range(1, m):
        full = full + s_recv[j]
    sim_ref[...] = full

    norm = jnp.zeros((CLS_PAD, 1), f32)
    for f in range(chunks):
        hi, lo = split(arrived(2, f, 0, n))
        part = dot(to_classes, hi) + dot(to_classes, lo)
        own[f] = part
        norm = norm + jnp.sum(part * part, axis=1, keepdims=True)
    length = jnp.sqrt(norm + epsilon)
    for f in range(chunks):
        proto_ref[:, f * CHUNK : (f + 1) * CHUNK] = (own[f] / length)[:CLS_DEV, :]

    def sent(target, to):
        cnt_copy(target, to, my_position).wait_send()
        for phase in range(3):
            for f in range(chunks):
                big_copy(phase, f, target, to, my_position).wait_send()

    for g in range(2):
        others(g, sent)
    for off in range(1, m):
        s_copy(off).wait_send()


def finish(means_ref, proto_ref, sim_ref, means_out, proto_out, sim_out, sems):
    copies = [
        pltpu.make_async_copy(means_ref, means_out, sems.at[0]),
        pltpu.make_async_copy(proto_ref, proto_out, sems.at[1]),
        pltpu.make_async_copy(sim_ref, sim_out, sems.at[2]),
    ]
    for copy in copies:
        copy.start()
    for copy in copies:
        copy.wait()


def shards(embeddings, labels, row_count):
    rows, width = embeddings.shape
    n = lax.axis_size("dp")
    m = lax.axis_size("cls")
    chunks = width // CHUNK
    slots = n * SLOTS
    vmem = pl.BlockSpec(memory_space=pltpu.VMEM)
    anywhere = pl.BlockSpec(memory_space=pl.ANY)
    exchange_buffer = pltpu.VMEM((chunks, n, SLOTS, CHUNK), f32)
    dma = pltpu.SemaphoreType.DMA
    results = (
        jax.ShapeDtypeStruct((CLS_DEV, width), f32),
        jax.ShapeDtypeStruct((CLS_DEV, width), f32),
        jax.ShapeDtypeStruct((1, rows), f32),
    )
    held = pl.pallas_call(
        functools.partial(kernel, n, m),
        out_shape=results,
        in_specs=[
            pl.BlockSpec(memory_space=pltpu.SMEM),
            vmem,
            pl.BlockSpec(memory_space=pltpu.HBM),
        ],
        out_specs=(vmem, vmem, vmem),
        scratch_shapes=[
            pltpu.VMEM((chunks, rows, CHUNK), bf16),
            pltpu.VMEM((slots, rows), bf16),
            pltpu.VMEM((slots // 2, rows), bf16),
            pltpu.VMEM((slots, CLS_PAD), f32),
            pltpu.VMEM((n, 8, CLS_PAD), f32),
            pltpu.VMEM((n, 8, CLS_PAD), f32),
            exchange_buffer,
            exchange_buffer,
            exchange_buffer,
            exchange_buffer,
            exchange_buffer,
            exchange_buffer,
            pltpu.VMEM((1, rows), f32),
            pltpu.VMEM((m, 1, rows), f32),
            pltpu.VMEM((1, rows), f32),
            pltpu.VMEM((1, rows), f32),
            pltpu.VMEM((chunks, CLS_PAD, CHUNK), f32),
            dma((chunks,)),
            dma((n,)),
            dma((n,)),
            dma((3, chunks, n)),
            dma((3, chunks, n)),
            dma((m - 1,)),
            dma((m - 1,)),
        ],
        compiler_params=pltpu.CompilerParams(
            collective_id=0, has_side_effects=True, vmem_limit_bytes=32 * 1024 * 1024
        ),
    )(row_count, labels.reshape(1, rows), embeddings)
    means, protos, similarity = pl.pallas_call(
        finish,
        out_shape=results,
        in_specs=[anywhere] * 3,
        out_specs=(anywhere,) * 3,
        scratch_shapes=[pltpu.SemaphoreType.DMA((3,))],
        compiler_params=pltpu.CompilerParams(vmem_limit_bytes=1024 * 1024),
    )(*held)
    return (means, protos, similarity.reshape(rows))


def solution(mesh):
    in_specs = (P("dp", None), P("dp"), P("dp"))
    out_specs = (P(("dp", "cls"), None), P(("dp", "cls"), None), P("dp"))
    return jax.shard_map(shards, mesh=mesh, in_specs=in_specs, out_specs=out_specs, check_vma=False)
```

profile of v0, /device:TPU:0, one launch (start us, length us, event | category | flops | bytes accessed | tf_op | source)
XLA Modules:
  0.0 39.9 jit_solution(10412555006150170624)
XLA Ops:
  1.3 0.0 copy-start
  1.3 2.3 %copy-done = bf16[3072,768]{1,0:T(8,128)(2,1)S(1)} copy-done((bf16[3072,768]{1,0:T(8,128)(2,1)S(1)}, bf16[3072,768]{1,0:T(8,128)(2,1)}, u32[]{:S(2)}) %copy-start) | copy-done | bytes 4718616
  3.6 0.0 copy-start.1
  3.6 0.7 %copy-done.1 = s32[3072]{0:T(1024)S(1)} copy-done((s32[3072]{0:T(1024)S(1)}, s32[3072]{0:T(1024)}, u32[]{:S(2)}) %copy-start.1) | copy-done | bytes 12312
  4.3 34.7 %shard_map.58 = (f32[86,768]{1,0:T(8,128)S(1)}, f32[86,768]{1,0:T(8,128)S(1)}, f32[1,3072]{1,0:T(1,128)S(1)}) custom-call(s32[1]{0:T(128)S(6)} %copy.6.count_ref, s32[1,3072]{1,0:T(1,128)S(1)} %bitcast.2, bf16[3072,768]{1,0:T(8,128)(2,1)S(1)} %copy-done), custom_call_target="tpu_custom_call" | custom-call | tf_op jit(solution)/shard_map/pallas_call | solution.py:326
  39.1 0.8 %shard_map.59 = (f32[86,768]{1,0:T(8,128)}, f32[86,768]{1,0:T(8,128)}, f32[1,3072]{1,0:T(1,128)}) custom-call(f32[86,768]{1,0:T(8,128)S(1)} %get-tuple-element.9.means_ref, f32[86,768]{1,0:T(8,128)S(1)} %get-tuple-element.10.proto_ref, f32[1,3072]{1,0:T(1,128)S(1)} %get-tuple-element.11.sim_ref), custom_call_target="tpu_custom_call" | custom-call | tf_op jit(solution)/shard_map/pallas_call | solution.py:365
Async XLA Ops:
  1.3 2.3 %copy-start = (bf16[3072,768]{1,0:T(8,128)(2,1)S(1)}, bf16[3072,768]{1,0:T(8,128)(2,1)}, u32[]{:S(2)}) copy-start(bf16[3072,768]{1,0:T(8,128)(2,1)} %emb_ref.1) | copy-start | bytes 14155780
  3.6 0.7 %copy-start.1 = (s32[3072]{0:T(1024)S(1)}, s32[3072]{0:T(1024)}, u32[]{:S(2)}) copy-start(s32[3072]{0:T(1024)} %param.4) | copy-start | bytes 36868
where the time goes:
time: 40.5 us; the launch traced here: 39.9 us
  Pallas kernels  35.6 us (88%)
  local copies, waits for them, and re-layouts  3.04 us (8%)
  between operations  1.29 us (3%)
    pallas_call x1, Pallas kernels, shards(): pl.pallas_call(functools.partial(kernel, n, m), out_shape=results, in_spe...  34.7 us
    unnamed x4, local copies, waits for them, and re-layouts  3.04 us
    pallas_call x1, Pallas kernels, shards(): pl.pallas_call(finish, out_shape=results, in_specs=[anywhere] * 3, out_sp...  0.82 us

commit v1 on v0

--- a/solution.py
+++ b/solution.py
@@ -44,6 +44,7 @@
     means_ref,
     proto_ref,
     sim_ref,
+    label_rows,
     emb,
     onehot,
     weighted_onehot,
@@ -61,6 +62,7 @@
     dot_row,
     len_row,
     own,
+    label_sem,
     load_sem,
     cnt_ss,
     cnt_rs,
@@ -88,6 +90,8 @@
             z = lax.rem(my_z + off, half)
             yield index_of(g, z), g * half + z
 
+    label_load = pltpu.make_async_copy(label_ref, label_rows, label_sem)
+    label_load.start()
     loads = []
     for f in range(chunks):
         load = pltpu.make_async_copy(
@@ -106,7 +110,8 @@
             barrier, inc=1, device_id={"cls": lax.rem(mine + off, m)}, device_id_type=pl.DeviceIdType.MESH
         )
 
-    label = label_ref[...].astype(f32)
+    label_load.wait()
+    label = label_rows[...].astype(f32)
     block = jnp.floor((label + 0.5) * (1.0 / CLS_DEV))
     place = label - CLS_DEV * block
     owner = jnp.floor((block + 0.5) * (1.0 / m))
@@ -328,11 +333,12 @@
         out_shape=results,
         in_specs=[
             pl.BlockSpec(memory_space=pltpu.SMEM),
-            vmem,
+            pl.BlockSpec(memory_space=pltpu.HBM),
             pl.BlockSpec(memory_space=pltpu.HBM),
         ],
         out_specs=(vmem, vmem, vmem),
         scratch_shapes=[
+            pltpu.VMEM((1, rows), jnp.int32),
             pltpu.VMEM((chunks, rows, CHUNK), bf16),
             pltpu.VMEM((slots, rows), bf16),
             pltpu.VMEM((slots // 2, rows), bf16),
@@ -350,6 +356,7 @@
             pltpu.VMEM((1, rows), f32),
             pltpu.VMEM((1, rows), f32),
             pltpu.VMEM((chunks, CLS_PAD, CHUNK), f32),
+            dma,
             dma((chunks,)),
             dma((n,)),
             dma((n,)),
@@ -361,7 +368,11 @@
         compiler_params=pltpu.CompilerParams(
             collective_id=0, has_side_effects=True, vmem_limit_bytes=32 * 1024 * 1024
         ),
-    )(row_count, labels.reshape(1, rows), embeddings)
+    )(
+        row_count,
+        pltpu.with_memory_space_constraint(labels.reshape(1, rows), pltpu.HBM),
+        pltpu.with_memory_space_constraint(embeddings, pltpu.HBM),
+    )
     means, protos, similarity = pl.pallas_call(
         finish,
         out_shape=results,

time: 40.5 us -> 36.6 us (0.904)
  the two profiles are of different devices: /device:TPU:0 before, /device:TPU:9 now
where the time goes in v1:
time: 36.6 us; the launch traced here: 36.4 us
  Pallas kernels  35.1 us (96%)
  between operations  1.28 us (3%)
    pallas_call x1, Pallas kernels, shards(): pl.pallas_call(functools.partial(kernel, n, m), out_shape=results, in_spe...  34.3 us
    pallas_call x1, Pallas kernels, shards(): pl.pallas_call(finish, out_shape=results, in_specs=[anywhere] * 3, out_sp...  0.82 us

profile of v1, /device:TPU:9, one launch (start us, length us, event | category | flops | bytes accessed | tf_op | source)
XLA Modules:
  0.0 36.4 jit_solution(4678621245201179500)
XLA Ops:
  1.3 34.3 %shard_map.58 = (f32[86,768]{1,0:T(8,128)S(1)}, f32[86,768]{1,0:T(8,128)S(1)}, f32[1,3072]{1,0:T(1,128)S(1)}) custom-call(s32[1]{0:T(128)S(6)} %copy.6.count_ref, s32[1,3072]{1,0:T(1,128)} %bitcast.2, bf16[3072,768]{1,0:T(8,128)(2,1)} %emb_ref.1), custom_call_target="tpu_custom_call" | custom-call | tf_op jit(solution)/shard_map/pallas_call | solution.py:331
  35.6 0.8 %shard_map.59 = (f32[86,768]{1,0:T(8,128)}, f32[86,768]{1,0:T(8,128)}, f32[1,3072]{1,0:T(1,128)}) custom-call(f32[86,768]{1,0:T(8,128)S(1)} %get-tuple-element.9.means_ref, f32[86,768]{1,0:T(8,128)S(1)} %get-tuple-element.10.proto_ref, f32[1,3072]{1,0:T(1,128)S(1)} %get-tuple-element.11.sim_ref), custom_call_target="tpu_custom_call" | custom-call | tf_op jit(solution)/shard_map/pallas_call | solution.py:376

commit v2 on v1

v2 whole, which is shorter than its diff:
```python
import functools

import jax
import jax.numpy as jnp
from jax import lax
from jax.experimental import pallas as pl
from jax.experimental.pallas import tpu as pltpu
from jax.sharding import PartitionSpec as P

CLS_DEV = 86
SLOTS = 16
CLS_PAD = 128
CHUNK = 384
ROW_TILE = 512

epsilon = 1e-06
sharpness = 4.0

f32 = jnp.float32
bf16 = jnp.bfloat16
NN = (((1,), (0,)), ((), ()))
NT = (((1,), (1,)), ((), ()))


def dot(a, b, dims=NN):
    return lax.dot_general(a, b, dims, preferred_element_type=f32)


def split(x):
    hi = x.astype(bf16)
    return hi, (x - hi.astype(f32)).astype(bf16)


def iota(shape, dim):
    return lax.broadcasted_iota(jnp.int32, shape, dim).astype(f32)


def plan(n):
    half = n // 2
    cut = max(1, half // 4)
    items = list(range(half)) + sorted(range(half, n), key=lambda k: (-(k // 2), k % 2))
    groups = [(0, half + cut), (half + cut, half + 2 * cut), (half + 2 * cut, n)]
    order = [half - 1] + list(range(half, n - 1)) + list(range(1, half - 1)) + [n - 1]
    return items, groups, order


def kernel(
    n,
    m,
    count_hbm,
    label_ref,
    emb_ref,
    means_out,
    proto_out,
    sim_out,
    count_ref,
    means_ref,
    proto_ref,
    sim_ref,
    label_rows,
    emb,
    onehot,
    weighted_onehot,
    place_t,
    cnt_send,
    cnt_recv,
    a_send,
    a_recv,
    b_send,
    b_recv,
    c_send,
    c_recv,
    s_send,
    s_recv,
    dot_row,
    len_row,
    own,
    out_sems,
    count_sem,
    label_sem,
    load_sem,
    cnt_ss,
    cnt_rs,
    big_ss,
    big_rs,
    s_ss,
    s_rs,
):
    rows = label_ref.shape[1]
    chunks = emb.shape[0]
    slots = n * SLOTS
    me = lax.axis_index("dp")
    mine = lax.axis_index("cls")
    items, groups, order = plan(n)

    def partner(p):
        target, bit = me, 1
        while bit < n:
            if items[p] & bit:
                target = target + bit - 2 * bit * lax.rem(lax.div(me, bit), 2)
            bit *= 2
        return target

    label_load = pltpu.make_async_copy(label_ref, label_rows, label_sem)
    label_load.start()
    count_load = pltpu.make_async_copy(count_hbm, count_ref, count_sem)
    count_load.start()
    barrier = pltpu.get_barrier_semaphore()
    for p in range(1, n):
        pl.semaphore_signal(
            barrier, inc=1, device_id={"dp": partner(p)}, device_id_type=pl.DeviceIdType.MESH
        )
    for off in range(1, m):
        pl.semaphore_signal(
            barrier, inc=1, device_id={"cls": lax.rem(mine + off, m)}, device_id_type=pl.DeviceIdType.MESH
        )
    loads = []
    for f in range(chunks):
        load = pltpu.make_async_copy(
            emb_ref.at[:, pl.ds(f * CHUNK, CHUNK)], emb.at[f], load_sem.at[f]
        )
        load.start()
        loads.append(load)

    position = lax.broadcasted_iota(jnp.int32, (n, rows), 0)
    peers = jnp.zeros((n, rows), f32)
    for p in range(n):
        peers = jnp.where(position == p, partner(p).astype(f32), peers)

    count_load.wait()
    label_load.wait()
    label = label_rows[...].astype(f32)
    block = jnp.floor((label + 0.5) * (1.0 / CLS_DEV))
    place = label - CLS_DEV * block
    owner = jnp.floor((block + 0.5) * (1.0 / m))
    group = block - m * owner
    alive = lax.broadcasted_iota(jnp.int32, (1, rows), 1) < count_ref[0]
    owned = (group == mine.astype(f32)) & alive
    place = jnp.where(owned, place, -1.0)
    owner = jnp.where(owned, owner, -1.0)

    owner_mask = peers == owner
    place_hot = jnp.where(iota((CLS_PAD, rows), 0) == place, 1.0, 0.0).astype(bf16)
    counts = dot(jnp.where(owner_mask, 1.0, 0.0).astype(bf16), place_hot, NT)
    upper = jnp.where(
        iota((CLS_PAD, CLS_PAD), 0) <= iota((CLS_PAD, CLS_PAD), 1), 1.0, 0.0
    ).astype(bf16)

    def ranks(table):
        return dot(jnp.where(table > 0, 1.0, 0.0).astype(bf16), upper) - 1.0

    for p in range(n):
        cnt_send[p] = counts[p : p + 1, :]
    cnt_recv[0] = cnt_send[0]

    rank_of = dot(ranks(counts).astype(bf16), place_hot) + SLOTS * iota((n, rows), 0)
    slot = jnp.sum(jnp.where(owner_mask, rank_of, 0.0), axis=0, keepdims=True)
    slot = jnp.where(owned, slot, -1.0)
    onehot[...] = jnp.where(iota((slots, rows), 0) == slot, 1.0, 0.0).astype(bf16)

    def dp_copy(p, src, dst, send_sem, recv_sem):
        return pltpu.make_async_remote_copy(
            src_ref=src,
            dst_ref=dst,
            send_sem=send_sem,
            recv_sem=recv_sem,
            device_id={"dp": partner(p)},
            device_id_type=pl.DeviceIdType.MESH,
        )

    def cnt_copy(p, count=1):
        span = pl.ds(p, count)
        return dp_copy(p, cnt_send.at[span], cnt_recv.at[span], cnt_ss, cnt_rs)

    buffers = ((a_send, a_recv), (b_send, b_recv), (c_send, c_recv))

    def big_copy(phase, f, p, g=0):
        out, recv = buffers[phase]
        return dp_copy(p, out.at[f, p], recv.at[f, p], big_ss.at[phase], big_rs.at[phase, f, g])

    def piece(phase, f, g, first, stop):
        out, recv = buffers[phase]
        span = pl.ds(max(first, 1), stop - max(first, 1))
        return dp_copy(
            max(first, 1), out.at[f, span], recv.at[f, span], big_ss.at[phase], big_rs.at[phase, f, g]
        )

    def send(phase, f, positions, g=0):
        for p in positions:
            if p > 0:
                big_copy(phase, f, p, g).start()

    def keep(phase, f):
        out, recv = buffers[phase]
        recv[f, 0] = out[f, 0]

    def arrived(phase, f, g=0, first=0, stop=n):
        piece(phase, f, g, first, stop).wait_recv()
        return buffers[phase][1][f, first:stop].reshape((stop - first) * SLOTS, CHUNK)

    loads[0].wait()
    a_send[0] = dot(onehot[...], emb[0]).reshape(n, SLOTS, CHUNK)
    pl.semaphore_wait(barrier, n - 1 + m - 1)
    for p in order:
        cnt_copy(p).start()
    send(0, 0, order)
    keep(0, 0)
    for f in range(1, chunks):
        loads[f].wait()
        a_send[f] = dot(onehot[...], emb[f]).reshape(n, SLOTS, CHUNK)
        send(0, f, order)
        keep(0, f)

    for t in range(0, rows, ROW_TILE):
        squares = jnp.zeros((ROW_TILE, 128), f32)
        for f in range(chunks):
            for k in range(0, CHUNK, 128):
                x = emb[f, t : t + ROW_TILE, k : k + 128].astype(f32)
                squares = squares + x * x
        total = jnp.sum(jnp.transpose(squares), axis=0, keepdims=True)
        len_row[:, t : t + ROW_TILE] = jnp.sqrt(total + epsilon)

    cnt_copy(1, n - 1).wait_recv()
    table = jnp.concatenate([cnt_recv[p] for p in range(n)], axis=0)
    table_rank = jnp.where(table > 0, ranks(table), -1.0)
    slot_iota = iota((SLOTS, CLS_PAD), 0)
    for p in range(n):
        place_t[p * SLOTS : (p + 1) * SLOTS, :] = jnp.where(
            table_rank[p : p + 1, :] == slot_iota, 1.0, 0.0
        )
    to_slots = place_t[...].astype(bf16)
    to_classes = jnp.transpose(place_t[...]).astype(bf16)
    own_counts = jnp.maximum(jnp.sum(table, axis=0, keepdims=True), 1.0)
    divisor = jnp.transpose(jnp.broadcast_to(own_counts, (CLS_PAD, CLS_PAD)))[:, 0:1]

    for f in range(chunks):
        hi, lo = split(arrived(0, f))
        means = (dot(to_classes, hi) + dot(to_classes, lo)) / divisor
        hi, lo = split(means)
        b_send[f] = (dot(to_slots, hi) + dot(to_slots, lo)).reshape(n, SLOTS, CHUNK)
        for g, (first, stop) in enumerate(groups):
            send(1, f, [p for p in order if first <= p < stop], g)
        keep(1, f)
        means_ref[:, f * CHUNK : (f + 1) * CHUNK] = means[:CLS_DEV, :]
    means_copy = pltpu.make_async_copy(means_ref, means_out, out_sems.at[0])
    means_copy.start()

    def project(f, g, first, stop, start):
        mean = arrived(1, f, g, first, stop)
        height = (stop - first) * SLOTS
        both = jnp.concatenate(split(mean), axis=0)
        for t in range(0, rows, ROW_TILE):
            cols = slice(t, t + ROW_TILE)
            product = dot(both, emb[f, cols, :], NT)
            product = product[:height, :] + product[height:, :]
            hot = onehot[first * SLOTS : stop * SLOTS, cols].astype(f32)
            product = jnp.sum(product * hot, axis=0, keepdims=True)
            dot_row[:, cols] = product if start else dot_row[:, cols] + product
        return jnp.sum(mean * mean, axis=1, keepdims=True)

    norms = [0.0] * len(groups)
    for f in range(chunks - 1):
        for g, (first, stop) in enumerate(groups):
            norms[g] = norms[g] + project(f, g, first, stop, f == 0 and g == 0)
    for g, (first, stop) in enumerate(groups):
        span = slice(first * SLOTS, stop * SLOTS)
        norm = norms[g] + project(chunks - 1, g, first, stop, chunks == 1 and g == 0)
        scale = 1.0 / jnp.sqrt(norm + epsilon)
        for t in range(0, rows, ROW_TILE):
            cols = slice(t, t + ROW_TILE)
            hot = onehot[span, cols].astype(f32)
            row_scale = jnp.sum(hot * scale, axis=0, keepdims=True)
            similarity = dot_row[:, cols] * row_scale / len_row[:, cols]
            s_send[:, cols] = similarity if g == 0 else s_send[:, cols] + similarity
            weight = jnp.exp(sharpness * (similarity - 1.0))
            weighted_onehot[span, cols] = (hot * weight).astype(bf16)
        for f in range(chunks):
            c_send[f, first:stop] = dot(weighted_onehot[span, :], emb[f]).reshape(
                stop - first, SLOTS, CHUNK
            )
            send(2, f, [p for p in order if first <= p < stop])
    for f in range(chunks):
        keep(2, f)

    def s_copy(off):
        return pltpu.make_async_remote_copy(
            src_ref=s_send,
            dst_ref=s_recv.at[off - 1],
            send_sem=s_ss,
            recv_sem=s_rs,
            device_id={"cls": lax.rem(mine + off, m)},
            device_id_type=pl.DeviceIdType.MESH,
        )

    for off in range(1, m):
        s_copy(off).start()
    pltpu.make_async_copy(s_recv, s_recv, s_rs).wait()
    full = s_send[...]
    for j in range(m - 1):
        full = full + s_recv[j]
    sim_ref[...] = full
    sim_copy = pltpu.make_async_copy(sim_ref, sim_out, out_sems.at[1])
    sim_copy.start()

    norm = jnp.zeros((CLS_PAD, 1), f32)
    for f in range(chunks):
        hi, lo = split(arrived(2, f))
        part = dot(to_classes, hi) + dot(to_classes, lo)
        own[f] = part
        norm = norm + jnp.sum(part * part, axis=1, keepdims=True)
    length = jnp.sqrt(norm + epsilon)
    for f in range(chunks):
        proto_ref[:, f * CHUNK : (f + 1) * CHUNK] = (own[f] / length)[:CLS_DEV, :]
    proto_copy = pltpu.make_async_copy(proto_ref, proto_out, out_sems.at[2])
    proto_copy.start()

    cnt_copy(1, n - 1).wait_send()
    for phase in range(3):
        for f in range(chunks):
            piece(phase, f, 0, 0, n).wait_send()
    pltpu.make_async_copy(s_recv, s_recv, s_ss).wait()
    for copy in (means_copy, sim_copy, proto_copy):
        copy.wait()


def finish(means_ref, proto_ref, sim_ref, means_out, proto_out, sim_out, sems):
    copies = [
        pltpu.make_async_copy(means_ref, means_out, sems.at[0]),
        pltpu.make_async_copy(proto_ref, proto_out, sems.at[1]),
        pltpu.make_async_copy(sim_ref, sim_out, sems.at[2]),
    ]
    for copy in copies:
        copy.start()
    for copy in copies:
        copy.wait()


def shards(embeddings, labels, row_count):
    rows, width = embeddings.shape
    n = lax.axis_size("dp")
    m = lax.axis_size("cls")
    chunks = width // CHUNK
    slots = n * SLOTS
    anywhere = pl.BlockSpec(memory_space=pl.ANY)
    exchange_buffer = pltpu.VMEM((chunks, n, SLOTS, CHUNK), f32)
    dma = pltpu.SemaphoreType.DMA
    results = (
        jax.ShapeDtypeStruct((CLS_DEV, width), f32),
        jax.ShapeDtypeStruct((CLS_DEV, width), f32),
        jax.ShapeDtypeStruct((1, rows), f32),
    )
    held = pl.pallas_call(
        functools.partial(kernel, n, m),
        out_shape=results,
        in_specs=[
            anywhere,
            pl.BlockSpec(memory_space=pltpu.HBM),
            pl.BlockSpec(memory_space=pltpu.HBM),
        ],
        out_specs=(anywhere,) * 3,
        scratch_shapes=[
            pltpu.SMEM((1,), jnp.int32),
            pltpu.VMEM((CLS_DEV, width), f32),
            pltpu.VMEM((CLS_DEV, width), f32),
            pltpu.VMEM((1, rows), f32),
            pltpu.VMEM((1, rows), jnp.int32),
            pltpu.VMEM((chunks, rows, CHUNK), bf16),
            pltpu.VMEM((slots, rows), bf16),
            pltpu.VMEM((slots, rows), bf16),
            pltpu.VMEM((slots, CLS_PAD), f32),
            pltpu.VMEM((n, 1, CLS_PAD), f32),
            pltpu.VMEM((n, 1, CLS_PAD), f32),
            exchange_buffer,
            exchange_buffer,
            exchange_buffer,
            exchange_buffer,
            exchange_buffer,
            exchange_buffer,
            pltpu.VMEM((1, rows), f32),
            pltpu.VMEM((m - 1, 1, rows), f32),
            pltpu.VMEM((1, rows), f32),
            pltpu.VMEM((1, rows), f32),
            pltpu.VMEM((chunks, CLS_PAD, CHUNK), f32),
            dma((3,)),
            dma,
            dma,
            dma((chunks,)),
            dma,
            dma,
            dma((3,)),
            dma((3, chunks, len(plan(n)[1]))),
            dma,
            dma,
        ],
        compiler_params=pltpu.CompilerParams(
            collective_id=0, has_side_effects=True, vmem_limit_bytes=32 * 1024 * 1024
        ),
    )(
        row_count,
        pltpu.with_memory_space_constraint(labels.reshape(1, rows), pltpu.HBM),
        pltpu.with_memory_space_constraint(embeddings, pltpu.HBM),
    )
    means, protos, similarity = pl.pallas_call(
        finish,
        out_shape=results,
        in_specs=[anywhere] * 3,
        out_specs=(anywhere,) * 3,
        scratch_shapes=[pltpu.SemaphoreType.DMA((3,))],
        compiler_params=pltpu.CompilerParams(vmem_limit_bytes=1024 * 1024),
    )(*held)
    return (means, protos, similarity.reshape(rows))


def solution(mesh):
    in_specs = (P("dp", None), P("dp"), P("dp"))
    out_specs = (P(("dp", "cls"), None), P(("dp", "cls"), None), P("dp"))
    return jax.shard_map(shards, mesh=mesh, in_specs=in_specs, out_specs=out_specs, check_vma=False)
```

time: 36.6 us -> 35.6 us (0.973)
  the two profiles are of different devices: /device:TPU:9 before, /device:TPU:0 now
where the time goes in v2:
time: 35.6 us; the launch traced here: 35.4 us
  Pallas kernels  34.1 us (96%)
  between operations  1.28 us (4%)
    pallas_call x1, Pallas kernels, shards(): pl.pallas_call(functools.partial(kernel, n, m), out_shape=results, in_spe...  33.3 us
    pallas_call x1, Pallas kernels, shards(): pl.pallas_call(finish, out_shape=results, in_specs=[anywhere] * 3, out_sp...  0.82 us

profile of v2, /device:TPU:0, one launch (start us, length us, event | category | flops | bytes accessed | tf_op | source)
XLA Modules:
  0.0 35.4 jit_solution(14495061642206535686)
XLA Ops:
  1.3 33.3 %shard_map.58 = (f32[86,768]{1,0:T(8,128)S(1)}, f32[86,768]{1,0:T(8,128)S(1)}, f32[1,3072]{1,0:T(1,128)S(1)}) custom-call(s32[1]{0:T(128)S(6)} %copy.6.count_hbm, s32[1,3072]{1,0:T(1,128)} %bitcast.2, bf16[3072,768]{1,0:T(8,128)(2,1)} %emb_ref.1), custom_call_target="tpu_custom_call" | custom-call | tf_op jit(solution)/shard_map/pallas_call | solution.py:352
  34.6 0.8 %shard_map.59 = (f32[86,768]{1,0:T(8,128)}, f32[86,768]{1,0:T(8,128)}, f32[1,3072]{1,0:T(1,128)}) custom-call(f32[86,768]{1,0:T(8,128)S(1)} %get-tuple-element.9.means_ref, f32[86,768]{1,0:T(8,128)S(1)} %get-tuple-element.10.proto_ref, f32[1,3072]{1,0:T(1,128)S(1)} %get-tuple-element.11.sim_ref), custom_call_target="tpu_custom_call" | custom-call | tf_op jit(solution)/shard_map/pallas_call | solution.py:403

commit v3 on v2

--- a/solution.py
+++ b/solution.py
@@ -11,7 +11,7 @@
 SLOTS = 16
 CLS_PAD = 128
 CHUNK = 384
-ROW_TILE = 512
+ROW_TILE = 256
 
 epsilon = 1e-06
 sharpness = 4.0
@@ -207,9 +207,6 @@
     keep(0, 0)
     for f in range(1, chunks):
         loads[f].wait()
-        a_send[f] = dot(onehot[...], emb[f]).reshape(n, SLOTS, CHUNK)
-        send(0, f, order)
-        keep(0, f)
 
     for t in range(0, rows, ROW_TILE):
         squares = jnp.zeros((ROW_TILE, 128), f32)
@@ -219,6 +216,11 @@
                 squares = squares + x * x
         total = jnp.sum(jnp.transpose(squares), axis=0, keepdims=True)
         len_row[:, t : t + ROW_TILE] = jnp.sqrt(total + epsilon)
+
+    for f in range(1, chunks):
+        a_send[f] = dot(onehot[...], emb[f]).reshape(n, SLOTS, CHUNK)
+        send(0, f, order)
+        keep(0, f)
 
     cnt_copy(1, n - 1).wait_recv()
     table = jnp.concatenate([cnt_recv[p] for p in range(n)], axis=0)

time: 35.6 us -> 35.7 us (level)
  no operation moved by 1% of the time
where the time goes in v3:
time: 35.7 us; the launch traced here: 35.5 us
  Pallas kernels  34.2 us (96%)
  between operations  1.28 us (4%)
    pallas_call x1, Pallas kernels, shards(): pl.pallas_call(functools.partial(kernel, n, m), out_shape=results, in_spe...  33.4 us
    pallas_call x1, Pallas kernels, shards(): pl.pallas_call(finish, out_shape=results, in_specs=[anywhere] * 3, out_sp...  0.82 us

profile of v3, /device:TPU:0, one launch (start us, length us, event | category | flops | bytes accessed | tf_op | source)
XLA Modules:
  0.0 35.5 jit_solution(152656594511896337)
XLA Ops:
  1.3 33.4 %shard_map.58 = (f32[86,768]{1,0:T(8,128)S(1)}, f32[86,768]{1,0:T(8,128)S(1)}, f32[1,3072]{1,0:T(1,128)S(1)}) custom-call(s32[1]{0:T(128)S(6)} %copy.6.count_hbm, s32[1,3072]{1,0:T(1,128)} %bitcast.2, bf16[3072,768]{1,0:T(8,128)(2,1)} %emb_ref.1), custom_call_target="tpu_custom_call" | custom-call | tf_op jit(solution)/shard_map/pallas_call | solution.py:354
  34.7 0.8 %shard_map.59 = (f32[86,768]{1,0:T(8,128)}, f32[86,768]{1,0:T(8,128)}, f32[1,3072]{1,0:T(1,128)}) custom-call(f32[86,768]{1,0:T(8,128)S(1)} %get-tuple-element.9.means_ref, f32[86,768]{1,0:T(8,128)S(1)} %get-tuple-element.10.proto_ref, f32[1,3072]{1,0:T(1,128)S(1)} %get-tuple-element.11.sim_ref), custom_call_target="tpu_custom_call" | custom-call | tf_op jit(solution)/shard_map/pallas_call | solution.py:405
